TPU v7x, 8 devices: a whole 2x2x1 slice. The times are simulated.
8 devices in a mesh: fsdp: 8 (over z, y, x, core).
Axes of the slice: x: 2, y: 2, z: 1, core: 2. Of those that a mesh axis runs over, the one named last changes fastest.
Arguments:
- left_mat: bfloat16 [65536, 4096], P('fsdp')
- right_mat: bfloat16 [4096, 4096], P('fsdp')
Outputs:
- output: bfloat16 [65536, 4096], P('fsdp')
All inputs are finite; a program needn't handle non-finite values.
Results may differ from a plain program's by a relative error of at most 0.001.
Values are sent between devices in bfloat16 or wider.
A program may use at most 1 GiB of HBM per device.

v0:
```python
import jax
import jax.numpy as jnp
from jax import lax
from jax.sharding import PartitionSpec as P


def solution(mesh):
    spec_rows = P("fsdp", None)

    def local_fn(left_blk, right_blk):
        full_right = lax.all_gather(right_blk, "fsdp", axis=0, tiled=True)
        return jnp.dot(left_blk, full_right, preferred_element_type=jnp.float32).astype(jnp.bfloat16)

    return jax.shard_map(local_fn, mesh=mesh, in_specs=(spec_rows, spec_rows), out_specs=spec_rows, check_vma=False)
```

profile of v0, /device:TPU:0, one launch (start us, length us, event | category | flops | bytes accessed | tf_op | source)
XLA Modules:
  0.0 466.5 jit_solution(9289652370992861025)
XLA Ops:
  6.5 0.0 all-gather.2.cloned.1.call-start
  6.5 0.7 all-gather.2.cloned.1.call-update
  7.3 160.0 %all-gather.2.cloned.1.call-done = bf16[4096,4096]{1,0:T(8,128)(2,1)} async-done(((bf16[512,4096]{1,0:T(8,128)(2,1)}), bf16[4096,4096]{1,0:T(8,128)(2,1)}) %all-gather.2.cloned.1.call-update) | async-done | bytes 33554448 | tf_op jit(solution)/shard_map/all_gather | solution.py:11
  167.2 292.4 %convolution_convert_fusion = bf16[8192,4096]{1,0:T(8,128)(2,1)} fusion(bf16[8192,4096]{1,0:T(8,128)(2,1)} %param.2, bf16[4096,4096]{1,0:T(8,128)(2,1)} %all-gather.2.cloned.1.call-done), kind=kOutput, calls=%fused_computation | convolution fusion | flops 274911461376 | bytes 167772160 | tf_op jit(solution)/shard_map/dot_general | solution.py:12
Async XLA Ops:
  6.5 160.7 %all-gather.2.cloned.1.call-start = ((), (), s32[]{:S(2)}) async-start(), calls=%async_computation | async-start | bytes 37748736 | tf_op jit(solution)/shard_map/all_gather | solution.py:11
Sparse Core Ops, SparseCore 0:
  9.1 158.0 all-gather.1
where the time goes:
time: 467 us
  matrix products  292 us (63%)
  waiting for transfers between devices  161 us (34%)
  between operations  13.4 us (3%)
    dot_general x1, matrix products, local_fn(): jnp.dot(left_blk, full_right, preferred_element_type=jnp.float32)  292 us
    all_gather x1, waiting for transfers between devices, local_fn(): full_right = lax.all_gather(right_blk, 'fsdp', axis=0, tiled=True)  160 us
  transfers between devices with their start and end apart: 1, of which 1 were waited for; matrix products, arithmetic and copies ran while one was open for 0% of the time, Pallas kernels for 0%

commit v1 on v0

v1 whole, which is shorter than its diff:
```python
import jax
import jax.numpy as jnp
from jax import lax
from jax.experimental import pallas as pl
from jax.experimental.pallas import tpu as pltpu
from jax.sharding import PartitionSpec as P

MESH = pl.DeviceIdType.MESH
BM = 1024
CW = 256
JW = 512
F32 = jnp.float32
BF16 = jnp.bfloat16

KP, KX, KY, KXP, KYP, KDY, KDX, KDYP, KDXP = range(9)


def _gather_kernel(n1, a_hbm, b_hbm, c1_hbm, bh_hbm, bv, abuf, obuf, acc, own, ssem, rsem, asem, osem, lsem):
    m_rows, k_all = a_hbm.shape
    depth, n_all = b_hbm.shape
    nm = m_rows // BM
    pieces = n_all // CW
    nv = n1 // CW
    slab = 2 * depth
    half = depth // 2

    me = lax.axis_index("fsdp")
    chip = me // 2
    core = me % 2
    chip_x = chip + 1 - 2 * (chip % 2)
    chip_y = (chip + 2) % 4
    chip_d = 3 - chip
    partner = chip * 2 + 1 - core
    dev_x = chip_x * 2 + core
    dev_y = chip_y * 2 + core

    def chip_at(r):
        return (chip, chip_x, chip_y, chip_d)[r]

    barrier = pltpu.get_barrier_semaphore()
    for dev in (partner, dev_x, dev_y):
        pl.semaphore_signal(barrier, inc=1, device_id=(dev,), device_id_type=MESH)

    own_v = pltpu.make_async_copy(
        b_hbm.at[:, pl.ds(0, n1)], bv.at[pl.ds(pl.multiple_of(core * depth, depth), depth), :], lsem.at[0])
    own_h_in = pltpu.make_async_copy(b_hbm.at[:, pl.ds(n1, n_all - n1)], own, lsem.at[1])
    own_h_out = pltpu.make_async_copy(own, bh_hbm.at[pl.ds(pl.multiple_of(me * depth, depth), depth), :], lsem.at[2])

    def a_copy(m, r, slot, place):
        q = chip_at(r)
        return pltpu.make_async_copy(
            a_hbm.at[pl.ds(pl.multiple_of(m * BM, BM), BM), pl.ds(pl.multiple_of(q * slab, slab), slab)],
            abuf.at[slot, :, pl.ds(pl.multiple_of(place * slab, slab), slab)],
            asem.at[slot, place],
        )

    own_v.start()
    own_h_in.start()
    for m in range(8):
        a_copy(m, 0, m % 2, m // 2).start()

    pl.semaphore_wait(barrier, 3)

    def copy(kind, t, in_v):
        cols_b = pl.ds(pl.multiple_of(t * CW, CW), CW)
        buf = bv if in_v else bh_hbm
        cols = cols_b if in_v else pl.ds(pl.multiple_of((t - nv) * CW, CW), CW)

        def rows(r, c, first, size):
            base = (2 * r + c) if in_v else (2 * chip_at(r) + c)
            return pl.ds(pl.multiple_of(base * depth + first, half), size)

        own_src = b_hbm.at[:, cols_b]
        at = lambda r, c, first=0, size=depth: buf.at[rows(r, c, first, size), cols]
        if kind == KP:
            src, dst, dev = own_src, at(0, core), partner
        elif kind == KX:
            src, dst, dev = own_src, (at(1, core) if in_v else at(0, core)), dev_x
        elif kind == KY:
            src, dst, dev = own_src, (at(2, core) if in_v else at(0, core)), dev_y
        elif kind == KXP:
            src, dst, dev = at(1, core), at(1, core), partner
        elif kind == KYP:
            src, dst, dev = at(2, core), at(2, core), partner
        elif kind == KDY:
            src, dst, dev = at(1, core, 0, half), (at(3, core, 0, half) if in_v else at(1, core, 0, half)), dev_y
        elif kind == KDX:
            src, dst, dev = at(2, core, half, half), (at(3, core, half, half) if in_v else at(2, core, half, half)), dev_x
        elif kind == KDYP:
            src, dst, dev = at(3, core, 0, half), at(3, core, 0, half), partner
        else:
            src, dst, dev = at(3, core, half, half), at(3, core, half, half), partner
        return pltpu.make_async_remote_copy(
            src_ref=src, dst_ref=dst, send_sem=ssem.at[kind, t], recv_sem=rsem.at[kind, t],
            device_id=(dev,), device_id_type=MESH)

    def each(t, body):
        if isinstance(t, int):
            if 0 <= t < pieces:
                body(t < nv)
            return

        @pl.when(t < nv)
        def _():
            body(True)

        @pl.when(jnp.logical_and(t >= nv, t < pieces))
        def _():
            body(False)

    def stage_a(t):
        def body(in_v):
            for kind in (KX, KY, KP):
                copy(kind, t, in_v).start()
        each(t, body)

    def stage_b(t):
        def body(in_v):
            copy(KX, t, in_v).wait_recv()
            copy(KDY, t, in_v).start()
            copy(KXP, t, in_v).start()
            copy(KY, t, in_v).wait_recv()
            copy(KDX, t, in_v).start()
            copy(KYP, t, in_v).start()
        each(t, body)

    def stage_c(t):
        def body(in_v):
            copy(KDY, t, in_v).wait_recv()
            copy(KDYP, t, in_v).start()
            copy(KDX, t, in_v).wait_recv()
            copy(KDXP, t, in_v).start()
        each(t, body)

    def landed(t, kinds):
        each(t, lambda in_v: [copy(kind, t, in_v).wait_recv() for kind in kinds])

    def out_copy(m, j, slot):
        return pltpu.make_async_copy(
            obuf.at[slot],
            c1_hbm.at[pl.ds(pl.multiple_of(m * BM, BM), BM), pl.ds(pl.multiple_of(j * JW, JW), JW)],
            osem.at[slot])

    def dot(x, y):
        return jnp.dot(x, y, preferred_element_type=F32)

    stage_a(0)
    stage_a(1)
    own_v.wait()
    landed(0, (KP,))
    landed(1, (KP,))

    def g0(m, carry):
        slot, place = m % 2, m // 2
        a_copy(m, 0, slot, place).wait()

        @pl.when(m == 5)
        def _():
            stage_b(0)

        @pl.when(m == 7)
        def _():
            for r in (1, 2):
                a_copy(0, r, 0, r).start()

        acc[pl.ds(pl.multiple_of(m * BM, BM), BM), :] = dot(
            abuf[slot, :, pl.ds(pl.multiple_of(place * slab, slab), slab)], bv[0:slab, 0:JW])
        return carry

    lax.fori_loop(0, nm, g0, 0)
    stage_b(1)
    stage_a(2)
    landed(0, (KXP, KYP))
    landed(1, (KXP, KYP))

    def g1(m, carry):
        slot = m % 2
        for r in (1, 2):
            a_copy(m, r, slot, r).wait()

        @pl.when(m < nm - 1)
        def _():
            for r in (1, 2):
                a_copy(m + 1, r, 1 - slot, r).start()

        @pl.when(m == 3)
        def _():
            stage_c(0)
            stage_a(3)

        @pl.when(m == 6)
        def _():
            stage_c(1)
            stage_b(2)
            stage_a(4)
            for i in range(4):
                a_copy(i, 3, i % 2, (3, 0)[i // 2]).start()

        @pl.when(m == 7)
        def _():
            a_copy(4, 3, 0, 1).start()
        rows = pl.ds(pl.multiple_of(m * BM, BM), BM)
        acc[rows, :] += dot(abuf[slot, :, slab:3 * slab], bv[slab:3 * slab, 0:JW])
        return carry

    lax.fori_loop(0, nm, g1, 0)
    own_h_in.wait()
    own_h_out.start()
    landed(0, (KDYP, KDXP))
    landed(1, (KDYP, KDXP))
    a_copy(5, 3, 1, 1).start()
    a_copy(6, 3, 0, 2).start()
    a_copy(7, 3, 1, 2).start()

    def g2(m, carry):
        slot, place = m % 2, (3 + m // 2) % 4
        a_copy(m, 3, slot, place).wait()

        @pl.when(m == 3)
        def _():
            a_copy(0, 3, 0, 3).start()
            a_copy(0, 0, 0, 0).start()

        @pl.when(m == 5)
        def _():
            a_copy(0, 1, 0, 1).start()
            stage_b(3)
            stage_a(5)
            stage_c(2)

        @pl.when(m == 7)
        def _():
            a_copy(0, 2, 0, 2).start()

        @pl.when(m >= 2)
        def _():
            out_copy(m - 2, 0, slot).wait()
        rows = pl.ds(pl.multiple_of(m * BM, BM), BM)
        obuf[slot] = (acc[rows, :] + dot(abuf[slot, :, pl.ds(pl.multiple_of(place * slab, slab), slab)],
                                         bv[3 * slab:, 0:JW])).astype(BF16)
        out_copy(m, 0, slot).start()
        return carry

    lax.fori_loop(0, nm, g2, 0)

    jobs = n1 // JW
    steps = nm * (jobs - 1)

    def step(s, carry):
        m, j, slot = s % nm, 1 + s // nm, s % 2
        for r in range(4):
            a_copy(m, r, slot, r).wait()

        @pl.when(s < steps - 1)
        def _():
            for r in range(4):
                a_copy((s + 1) % nm, r, 1 - slot, r).start()

        @pl.when(s % 2 == 0)
        def _():
            u = s // 2
            stage_b(4 + u)
            stage_a(6 + u)
            stage_c(3 + u)

        @pl.when(m == 0)
        def _():
            for i in range(2):
                for kind in (KP, KXP, KYP, KDYP, KDXP):
                    copy(kind, 2 * j + i, True).wait_recv()

        out_copy(m, j, slot).wait()
        obuf[slot] = dot(abuf[slot], bv[:, pl.ds(pl.multiple_of(j * JW, JW), JW)]).astype(BF16)
        out_copy(m, j, slot).start()
        return carry

    lax.fori_loop(0, steps, step, 0)
    for t in range(4 + steps // 2, pieces):
        stage_b(t)
    for t in range(3 + steps // 2, pieces):
        stage_c(t)

    def rest(t, carry):
        for kind in (KP, KXP, KYP, KDYP, KDXP):
            copy(kind, t, False).wait_recv()
        return carry

    lax.fori_loop(nv, pieces, rest, 0)

    def sent(in_v):
        def body(t, carry):
            for kind in range(9):
                copy(kind, t, in_v).wait_send()
            return carry
        return body

    lax.fori_loop(0, nv, sent(True), 0)
    lax.fori_loop(nv, pieces, sent(False), 0)
    own_h_out.wait()
    for slot in range(2):
        out_copy(0, 0, slot).wait()


def _rest_kernel(n1, bn, a_ref, b_ref, c1_hbm, c_hbm, obuf, cbuf, osem, isem, xsem):
    n, m = pl.program_id(0), pl.program_id(1)
    nm = pl.num_programs(1)
    steps = pl.num_programs(0) * nm
    s = n * nm + m
    slot = s % 2
    rows = c1_hbm.shape[0] // (2 * nm)

    def take(i, k):
        return pltpu.make_async_copy(c1_hbm.at[pl.ds(pl.multiple_of(i * rows, rows), rows), :], cbuf.at[k], isem.at[k])

    def put(i, k):
        return pltpu.make_async_copy(
            cbuf.at[k], c_hbm.at[pl.ds(pl.multiple_of(i * rows, rows), rows), pl.ds(0, n1)], xsem.at[k])

    def out(k):
        return pltpu.make_async_copy(
            obuf.at[k],
            c_hbm.at[pl.ds(pl.multiple_of(m * BM, BM), BM), pl.ds(pl.multiple_of(n1 + n * bn, bn), bn)],
            osem.at[k])

    @pl.when(s == 0)
    def _():
        take(0, 0).start()

    take(s, slot).wait()
    put(s, slot).start()

    @pl.when(s >= 1)
    def _():
        put(s - 1, 1 - slot).wait()

    @pl.when(s < steps - 1)
    def _():
        take(s + 1, 1 - slot).start()

    @pl.when(s >= 2)
    def _():
        out(slot).wait()

    obuf[slot] = jnp.dot(a_ref[...], b_ref[...], preferred_element_type=F32).astype(BF16)
    out(slot).start()

    @pl.when(s == steps - 1)
    def _():
        put(s, slot).wait()
        out(1 - slot).wait()
        out(slot).wait()


def solution(mesh):
    def local_fn(a, b):
        m_rows, k_all = a.shape
        depth, n_all = b.shape
        n1 = n_all // 2
        pieces = n_all // CW
        any_spec = pl.BlockSpec(memory_space=pl.ANY)
        c1, bh = pl.pallas_call(
            lambda *refs: _gather_kernel(n1, *refs),
            out_shape=(jax.ShapeDtypeStruct((m_rows, n1), BF16), jax.ShapeDtypeStruct((k_all, n_all - n1), BF16)),
            in_specs=[any_spec, any_spec],
            out_specs=(any_spec, any_spec),
            scratch_shapes=[
                pltpu.VMEM((k_all, n1), BF16),
                pltpu.VMEM((2, BM, k_all), BF16),
                pltpu.VMEM((2, BM, JW), BF16),
                pltpu.VMEM((m_rows, JW), F32),
                pltpu.VMEM((depth, n_all - n1), BF16),
                pltpu.SemaphoreType.DMA((9, pieces)),
                pltpu.SemaphoreType.DMA((9, pieces)),
                pltpu.SemaphoreType.DMA((2, 4)),
                pltpu.SemaphoreType.DMA((2,)),
                pltpu.SemaphoreType.DMA((3,)),
            ],
            compiler_params=pltpu.CompilerParams(
                collective_id=0, has_side_effects=True, vmem_limit_bytes=63 * 1024 * 1024),
            cost_estimate=pl.CostEstimate(
                flops=2 * m_rows * k_all * n1, bytes_accessed=6 * m_rows * k_all, transcendentals=0),
            name="gather_half",
        )(a, b)
        bn = 1024
        nm = m_rows // BM
        return pl.pallas_call(
            lambda *refs: _rest_kernel(n1, bn, *refs),
            grid=((n_all - n1) // bn, nm),
            out_shape=jax.ShapeDtypeStruct((m_rows, n_all), BF16),
            in_specs=[
                pl.BlockSpec((BM, k_all), lambda n, m: (m, 0)),
                pl.BlockSpec((k_all, bn), lambda n, m: (0, n)),
                any_spec,
            ],
            out_specs=any_spec,
            scratch_shapes=[
                pltpu.VMEM((2, BM, bn), BF16),
                pltpu.VMEM((2, m_rows // (2 * nm), n1), BF16),
                pltpu.SemaphoreType.DMA((2,)),
                pltpu.SemaphoreType.DMA((2,)),
                pltpu.SemaphoreType.DMA((2,)),
            ],
            compiler_params=pltpu.CompilerParams(vmem_limit_bytes=60 * 1024 * 1024),
            cost_estimate=pl.CostEstimate(
                flops=2 * m_rows * k_all * (n_all - n1), bytes_accessed=6 * m_rows * k_all, transcendentals=0),
            name="rest",
        )(a, bh, c1)

    spec = P("fsdp", None)
    return jax.shard_map(local_fn, mesh=mesh, in_specs=(spec, spec), out_specs=spec, check_vma=False)
```

time: 467 us -> 318 us (0.68)
  Pallas kernels: 0 us -> 317 us
  matrix products: 292 us -> 0 us
  waiting for transfers between devices: 161 us -> 0 us
  between operations: 13.4 us -> 0.01 us
    pallas_call x0 -> x2, Pallas kernels: none -> 317 us  [the longest x1 166 us: local_fn(): pl.pallas_call(lambda *refs: _gather_kernel(n1, *refs), out_shape=(jax.Sh...]
    dot_general x1 -> x0, matrix products: 292 us -> none  [local_fn(): jnp.dot(left_blk, full_right, preferred_element_type=jnp.float32)]
    all_gather x1 -> x0, waiting for transfers between devices: 160 us -> none  [local_fn(): full_right = lax.all_gather(right_blk, 'fsdp', axis=0, tiled=True)]
  transfers between devices with their start and end apart: 1 -> 0, of which waited for: 1 -> 0; matrix products, arithmetic and copies ran while one was open for 0% -> 0% of each run, Pallas kernels for 0% -> 0%
where the time goes in v1:
time: 318 us; the launch traced here: 317 us
  Pallas kernels  317 us (100%)
    pallas_call x1, Pallas kernels, local_fn(): pl.pallas_call(lambda *refs: _gather_kernel(n1, *refs), out_shape=(jax.Sh...  166 us
    pallas_call x1, Pallas kernels, local_fn(): pl.pallas_call(lambda *refs: _rest_kernel(n1, bn, *refs), grid=((n_all -...  152 us

profile of v1, /device:TPU:0, one launch (start us, length us, event | category | flops | bytes accessed | tf_op | source)
XLA Modules:
  0.0 317.4 jit_solution(3764256530442162074)
XLA Ops:
  0.0 165.7 %gather_half.1 = (bf16[8192,2048]{1,0:T(8,128)(2,1)}, bf16[4096,2048]{1,0:T(8,128)(2,1)}) custom-call(bf16[8192,4096]{1,0:T(8,128)(2,1)} %refs_0_.3, bf16[512,4096]{1,0:T(8,128)(2,1)} %refs_1_.1), custom_call_target="tpu_custom_call" | custom-call | flops 137438953472 | bytes 201326592 | tf_op jit(solution)/shard_map/gather_half/pallas_call | solution.py:361
  165.7 151.7 %rest.1 = bf16[8192,4096]{1,0:T(8,128)(2,1)} custom-call(bf16[8192,4096]{1,0:T(8,128)(2,1)} %refs_0_.3, bf16[4096,2048]{1,0:T(8,128)(2,1)} %get-tuple-element.7.refs_1_, bf16[8192,2048]{1,0:T(8,128)(2,1)} %get-tuple-element.8.refs_2_), custom_call_target="tpu_custom_call" | custom-call | flops 137438953472 | bytes 201326592 | tf_op jit(solution)/shard_map/rest/pallas_call | solution.py:386

commit v2 on v1

v2 whole, which is shorter than its diff:
```python
import jax
import jax.numpy as jnp
from jax import lax
from jax.experimental import pallas as pl
from jax.experimental.pallas import tpu as pltpu
from jax.sharding import PartitionSpec as P

MESH = pl.DeviceIdType.MESH
BM = 1024
CW = 256
JW = 512
F32 = jnp.float32
BF16 = jnp.bfloat16

KP, KX, KY, KXP, KYP, KDY, KDX, KDYP, KDXP = range(9)


def _gather_kernel(n1, a_hbm, b_hbm, c1_hbm, bh_hbm, bv, abuf, obuf, acc, ssem, rsem, asem, osem, lsem):
    m_rows, k_all = a_hbm.shape
    depth, n_all = b_hbm.shape
    nm = m_rows // BM
    pieces = n_all // CW
    nv = n1 // CW
    slab = 2 * depth
    half = depth // 2

    me = lax.axis_index("fsdp")
    chip = me // 2
    core = me % 2
    chip_x = chip + 1 - 2 * (chip % 2)
    chip_y = (chip + 2) % 4
    chip_d = 3 - chip
    partner = chip * 2 + 1 - core
    dev_x = chip_x * 2 + core
    dev_y = chip_y * 2 + core

    def chip_at(r):
        return (chip, chip_x, chip_y, chip_d)[r]

    barrier = pltpu.get_barrier_semaphore()
    for dev in (partner, dev_x, dev_y):
        pl.semaphore_signal(barrier, inc=1, device_id=(dev,), device_id_type=MESH)

    own_v = pltpu.make_async_copy(
        b_hbm.at[:, pl.ds(0, n1)], bv.at[pl.ds(pl.multiple_of(core * depth, depth), depth), :], lsem.at[0])
    wide = n1 - 2 * JW

    def own_h(k, out):
        col = pl.ds(k * wide, wide)
        stop = obuf.at[k, pl.ds(0, depth), :]
        if out:
            rows = pl.ds(pl.multiple_of(me * depth, depth), depth)
            return pltpu.make_async_copy(stop, bh_hbm.at[rows, col], lsem.at[3 + k])
        return pltpu.make_async_copy(b_hbm.at[:, pl.ds(n1 + k * wide, wide)], stop, lsem.at[1 + k])

    def a_copy(m, r, slot, place):
        q = chip_at(r)
        return pltpu.make_async_copy(
            a_hbm.at[pl.ds(pl.multiple_of(m * BM, BM), BM), pl.ds(pl.multiple_of(q * slab, slab), slab)],
            abuf.at[slot, :, pl.ds(pl.multiple_of(place * slab, slab), slab)],
            asem.at[slot, place],
        )

    own_v.start()
    for m in range(8):
        a_copy(m, 0, m % 2, m // 2).start()
    for k in range(2):
        own_h(k, False).start()

    pl.semaphore_wait(barrier, 3)

    def copy(kind, t, in_v):
        cols_b = pl.ds(pl.multiple_of(t * CW, CW), CW)
        buf = bv if in_v else bh_hbm
        cols = cols_b if in_v else pl.ds(pl.multiple_of((t - nv) * CW, CW), CW)

        def rows(r, c, first, size):
            base = (2 * r + c) if in_v else (2 * chip_at(r) + c)
            return pl.ds(pl.multiple_of(base * depth + first, half), size)

        own_src = b_hbm.at[:, cols_b]
        at = lambda r, c, first=0, size=depth: buf.at[rows(r, c, first, size), cols]
        if kind == KP:
            src, dst, dev = own_src, at(0, core), partner
        elif kind == KX:
            src, dst, dev = own_src, (at(1, core) if in_v else at(0, core)), dev_x
        elif kind == KY:
            src, dst, dev = own_src, (at(2, core) if in_v else at(0, core)), dev_y
        elif kind == KXP:
            src, dst, dev = at(1, core), at(1, core), partner
        elif kind == KYP:
            src, dst, dev = at(2, core), at(2, core), partner
        elif kind == KDY:
            src, dst, dev = at(1, core, 0, half), (at(3, core, 0, half) if in_v else at(1, core, 0, half)), dev_y
        elif kind == KDX:
            src, dst, dev = at(2, core, half, half), (at(3, core, half, half) if in_v else at(2, core, half, half)), dev_x
        elif kind == KDYP:
            src, dst, dev = at(3, core, 0, half), at(3, core, 0, half), partner
        else:
            src, dst, dev = at(3, core, half, half), at(3, core, half, half), partner
        return pltpu.make_async_remote_copy(
            src_ref=src, dst_ref=dst, send_sem=ssem.at[kind, t], recv_sem=rsem.at[kind, t],
            device_id=(dev,), device_id_type=MESH)

    def each(t, body):
        if isinstance(t, int):
            if 0 <= t < pieces:
                body(t < nv)
            return

        @pl.when(t < nv)
        def _():
            body(True)

        @pl.when(jnp.logical_and(t >= nv, t < pieces))
        def _():
            body(False)

    def stage_a(t):
        def body(in_v):
            for kind in (KP, KX, KY):
                copy(kind, t, in_v).start()
        each(t, body)

    def stage_b(t):
        def body(in_v):
            copy(KX, t, in_v).wait_recv()
            copy(KDY, t, in_v).start()
            copy(KXP, t, in_v).start()
            copy(KY, t, in_v).wait_recv()
            copy(KDX, t, in_v).start()
            copy(KYP, t, in_v).start()
        each(t, body)

    def stage_c(t):
        def body(in_v):
            copy(KDY, t, in_v).wait_recv()
            copy(KDYP, t, in_v).start()
            copy(KDX, t, in_v).wait_recv()
            copy(KDXP, t, in_v).start()
        each(t, body)

    def landed(t, kinds):
        each(t, lambda in_v: [copy(kind, t, in_v).wait_recv() for kind in kinds])

    def out_copy(m, col, width, slot):
        return pltpu.make_async_copy(
            obuf.at[slot, :, pl.ds(0, width)],
            c1_hbm.at[pl.ds(pl.multiple_of(m * BM, BM), BM), pl.ds(col, width)],
            osem.at[slot])

    def dot(x, y):
        return jnp.dot(x, y, preferred_element_type=F32)

    def pair(i):
        return pl.ds(pl.multiple_of(i * 2 * BM, 2 * BM), 2 * BM)

    def pair_of(place, width):
        x = abuf[:, :, pl.ds(pl.multiple_of(place * slab, slab), width)]
        return x.reshape(2 * BM, width)

    stage_a(0)
    stage_a(1)
    own_v.wait()
    landed(0, (KP,))
    landed(1, (KP,))

    def g0(i, carry):
        for slot in range(2):
            a_copy(2 * i + slot, 0, slot, i).wait()

        @pl.when(i == 2)
        def _():
            for slot in range(2):
                a_copy(slot, 1, slot, 0).start()
                a_copy(slot, 2, slot, 1).start()

        acc[pair(i), :] = dot(pair_of(i, slab), bv[0:slab, 0:JW])
        return carry

    lax.fori_loop(0, nm // 2, g0, 0)
    for k in range(2):
        own_h(k, False).wait()
        own_h(k, True).start()
    stage_b(0)
    stage_b(1)
    stage_a(2)
    stage_a(3)
    landed(0, (KXP, KYP))
    landed(1, (KXP, KYP))

    def g1(i, carry):
        place = 2 * (i % 2)
        for slot in range(2):
            a_copy(2 * i + slot, 1, slot, place).wait()
            a_copy(2 * i + slot, 2, slot, place + 1).wait()

        @pl.when(i < nm // 2 - 1)
        def _():
            for slot in range(2):
                a_copy(2 * i + 2 + slot, 1, slot, 2 - place).start()
                a_copy(2 * i + 2 + slot, 2, slot, 3 - place).start()

        @pl.when(i == 1)
        def _():
            stage_c(0)
            stage_c(1)

        @pl.when(i == 3)
        def _():
            stage_b(2)
            stage_a(4)
            for slot in range(2):
                a_copy(slot, 3, slot, 0).start()
                a_copy(2 + slot, 3, slot, 1).start()

        acc[pair(i), :] += dot(pair_of(place, 2 * slab), bv[slab:3 * slab, 0:JW])
        return carry

    lax.fori_loop(0, nm // 2, g1, 0)
    landed(0, (KDYP, KDXP))
    landed(1, (KDYP, KDXP))
    stage_b(3)
    stage_a(5)
    stage_c(2)
    for k in range(2):
        own_h(k, True).wait()

    def g2(i, carry):
        for slot in range(2):
            a_copy(2 * i + slot, 3, slot, i).wait()

        @pl.when(i == 0)
        def _():
            for slot in range(2):
                a_copy(4 + slot, 3, slot, 2).start()
            a_copy(6, 3, 1, 3).start()
            a_copy(0, 3, 0, 3).start()

        @pl.when(i == 1)
        def _():
            a_copy(0, 0, 0, 0).start()
            a_copy(7, 3, 1, 0).start()

        @pl.when(i == 2)
        def _():
            a_copy(0, 1, 0, 1).start()

        @pl.when(i >= 1)
        def _():
            for slot in range(2):
                out_copy(2 * i - 2 + slot, 0, JW, slot).wait()

        res = (acc[pair(i), :] + dot(pair_of(i, slab), bv[3 * slab:, 0:JW])).astype(BF16)
        obuf[:, :, 0:JW] = res.reshape(2, BM, JW)
        for slot in range(2):
            out_copy(2 * i + slot, 0, JW, slot).start()
        return carry

    lax.fori_loop(0, nm // 2 - 1, g2, 0)
    a_copy(0, 2, 0, 2).start()
    stage_b(4)
    stage_a(6)

    def g2_last(m, carry):
        slot, place = m % 2, 3 * (7 - m)
        a_copy(m, 3, 1, place).wait()
        out_copy(m - 2, 0, JW, slot).wait()
        rows = pl.ds(pl.multiple_of(m * BM, BM), BM)
        obuf[slot, :, 0:JW] = (acc[rows, :] + dot(
            abuf[1, :, pl.ds(pl.multiple_of(place * slab, slab), slab)], bv[3 * slab:, 0:JW])).astype(BF16)
        out_copy(m, 0, JW, slot).start()
        return carry

    lax.fori_loop(nm - 2, nm, g2_last, 0)

    def tiles(s, m, last):
        slot = s % 2
        for r in range(4):
            a_copy(m, r, slot, r).wait()

        def ahead():
            for r in range(4):
                a_copy((m + 1) % nm, r, 1 - slot, r).start()

        if last is None:
            ahead()
        else:
            pl.when(jnp.logical_not(last))(ahead)
        return slot

    def job1(m, carry):
        slot = tiles(m, m, None)
        h = m // 2

        @pl.when(m % 2 == 0)
        def _():
            stage_c(3 + h)

        @pl.when(m % 2 == 1)
        def _():
            @pl.when(m < nm - 1)
            def _():
                stage_b(5 + h)
            stage_a(7 + h)

        @pl.when(m == nm - 1)
        def _():
            stage_c(7)

        @pl.when(m == 0)
        def _():
            for t in (2, 3):
                landed(t, (KP, KXP, KYP, KDYP, KDXP))

        out_copy(m, JW, JW, slot).wait()
        obuf[slot, :, 0:JW] = dot(abuf[slot], bv[:, JW:2 * JW]).astype(BF16)
        out_copy(m, JW, JW, slot).start()
        return carry

    lax.fori_loop(0, nm, job1, 0)
    for t in range(4, 8):
        landed(t, (KP, KXP, KYP, KDYP, KDXP))
    def job2(m, carry):
        slot = tiles(m, m, m == nm - 1)
        stage_b(8 + m)
        stage_a(11 + m)

        @pl.when(m >= 2)
        def _():
            stage_c(6 + m)

        @pl.when(m == nm - 1)
        def _():
            stage_c(14)

        @pl.when(m < 2)
        def _():
            out_copy(m, JW, JW, slot).wait()

        @pl.when(m >= 2)
        def _():
            out_copy(m, 2 * JW, wide, slot).wait()

        obuf[slot] = dot(abuf[slot], bv[:, 2 * JW:]).astype(BF16)
        out_copy(m, 2 * JW, wide, slot).start()
        return carry

    lax.fori_loop(0, nm, job2, 0)
    stage_c(15)

    def rest(t, carry):
        for kind in (KP, KXP, KYP, KDYP, KDXP):
            copy(kind, t, False).wait_recv()
        return carry

    lax.fori_loop(nv, pieces, rest, 0)

    def sent(in_v):
        def body(t, carry):
            for kind in range(9):
                copy(kind, t, in_v).wait_send()
            return carry
        return body

    lax.fori_loop(0, nv, sent(True), 0)
    lax.fori_loop(nv, pieces, sent(False), 0)
    for slot in range(2):
        out_copy(0, 2 * JW, wide, slot).wait()


def _rest_kernel(n1, bn, a_hbm, b_hbm, c1_hbm, c_hbm, abuf, bbuf, obuf, acc, cbuf, asem, bsem, osem, isem, xsem):
    m_rows, k_all = a_hbm.shape
    nm = m_rows // BM
    steps = nm * (b_hbm.shape[1] // bn)
    rows = m_rows // steps
    slab = k_all // 4

    def take(i, k):
        return pltpu.make_async_copy(c1_hbm.at[pl.ds(pl.multiple_of(i * rows, rows), rows), :], cbuf.at[k], isem.at[k])

    def put(i, k):
        return pltpu.make_async_copy(
            cbuf.at[k], c_hbm.at[pl.ds(pl.multiple_of(i * rows, rows), rows), pl.ds(0, n1)], xsem.at[k])

    def out(s, k):
        m, n = s % nm, s // nm
        return pltpu.make_async_copy(
            obuf.at[k],
            c_hbm.at[pl.ds(pl.multiple_of(m * BM, BM), BM), pl.ds(pl.multiple_of(n1 + n * bn, bn), bn)],
            osem.at[k])

    def a_slab(r):
        return pltpu.make_async_copy(
            a_hbm.at[pl.ds(0, BM), pl.ds(pl.multiple_of(r * slab, slab), slab)],
            abuf.at[0, :, pl.ds(pl.multiple_of(r * slab, slab), slab)], asem.at[2 + r])

    def b_slab(r):
        return pltpu.make_async_copy(
            b_hbm.at[pl.ds(pl.multiple_of(r * slab, slab), slab), pl.ds(0, bn)],
            bbuf.at[0, pl.ds(pl.multiple_of(r * slab, slab), slab), :], bsem.at[1 + r])

    def a_tile(s, k):
        return pltpu.make_async_copy(
            a_hbm.at[pl.ds(pl.multiple_of((s % nm) * BM, BM), BM), :], abuf.at[k], asem.at[k])

    b_next = pltpu.make_async_copy(b_hbm.at[:, pl.ds(bn, bn)], bbuf.at[1], bsem.at[0])

    for r in range(4):
        a_slab(r).start()
        b_slab(r).start()
    a_tile(1, 1).start()
    take(0, 0).start()
    acc[...] = jnp.zeros_like(acc)

    def part(r):
        a_slab(r).wait()
        b_slab(r).wait()
        cols = pl.ds(pl.multiple_of(r * slab, slab), slab)
        return jnp.dot(abuf[0, :, cols], bbuf[0, cols, :], preferred_element_type=F32)

    def first(r, carry):
        acc[...] += part(r)
        return carry

    lax.fori_loop(0, 3, first, 0)
    obuf[0] = (acc[...] + part(3)).astype(BF16)
    out(0, 0).start()
    take(0, 0).wait()
    put(0, 0).start()

    def step(s, carry):
        k, c = s % 2, s % 3
        a_tile(s, k).wait()

        @pl.when(s < steps - 1)
        def _():
            a_tile(s + 1, 1 - k).start()

        @pl.when(s == 1)
        def _():
            b_next.start()

        @pl.when(s == nm)
        def _():
            b_next.wait()

        @pl.when(jnp.logical_and(s >= 3, s < steps - 1))
        def _():
            put(s - 3, c).wait()

        @pl.when(s < steps - 1)
        def _():
            take(s, c).start()

        @pl.when(s == steps - 2)
        def _():
            put(steps - 4, (steps - 1) % 3).wait()
            take(steps - 1, (steps - 1) % 3).start()

        @pl.when(s >= 2)
        def _():
            out(s - 2, k).wait()

        obuf[k] = jnp.dot(abuf[k], bbuf[s // nm], preferred_element_type=F32).astype(BF16)
        out(s, k).start()

        @pl.when(s < steps - 1)
        def _():
            take(s, c).wait()
            put(s, c).start()

        @pl.when(s == steps - 2)
        def _():
            take(steps - 1, (steps - 1) % 3).wait()
            put(steps - 1, (steps - 1) % 3).start()
        return carry

    lax.fori_loop(1, steps, step, 0)
    for i in range(steps - 3, steps):
        put(i, i % 3).wait()
    for s in (steps - 2, steps - 1):
        out(s, s % 2).wait()


def solution(mesh):
    def local_fn(a, b):
        m_rows, k_all = a.shape
        depth, n_all = b.shape
        n1 = n_all // 2
        pieces = n_all // CW
        any_spec = pl.BlockSpec(memory_space=pl.ANY)
        c1, bh = pl.pallas_call(
            lambda *refs: _gather_kernel(n1, *refs),
            out_shape=(jax.ShapeDtypeStruct((m_rows, n1), BF16), jax.ShapeDtypeStruct((k_all, n_all - n1), BF16)),
            in_specs=[any_spec, any_spec],
            out_specs=(any_spec, any_spec),
            scratch_shapes=[
                pltpu.VMEM((k_all, n1), BF16),
                pltpu.VMEM((2, BM, k_all), BF16),
                pltpu.VMEM((2, BM, n1 - 2 * JW), BF16),
                pltpu.VMEM((m_rows, JW), F32),
                pltpu.SemaphoreType.DMA((9, pieces)),
                pltpu.SemaphoreType.DMA((9, pieces)),
                pltpu.SemaphoreType.DMA((2, 4)),
                pltpu.SemaphoreType.DMA((2,)),
                pltpu.SemaphoreType.DMA((5,)),
            ],
            compiler_params=pltpu.CompilerParams(
                collective_id=0, has_side_effects=True, vmem_limit_bytes=63 * 1024 * 1024),
            cost_estimate=pl.CostEstimate(
                flops=2 * m_rows * k_all * n1, bytes_accessed=6 * m_rows * k_all, transcendentals=0),
            name="gather_half",
        )(a, b)
        bn = 1024
        nm = m_rows // BM
        return pl.pallas_call(
            lambda *refs: _rest_kernel(n1, bn, *refs),
            out_shape=jax.ShapeDtypeStruct((m_rows, n_all), BF16),
            in_specs=[any_spec, any_spec, any_spec],
            out_specs=any_spec,
            scratch_shapes=[
                pltpu.VMEM((2, BM, k_all), BF16),
                pltpu.VMEM((2, k_all, bn), BF16),
                pltpu.VMEM((2, BM, bn), BF16),
                pltpu.VMEM((BM, bn), F32),
                pltpu.VMEM((3, m_rows // (2 * nm), n1), BF16),
                pltpu.SemaphoreType.DMA((6,)),
                pltpu.SemaphoreType.DMA((5,)),
                pltpu.SemaphoreType.DMA((2,)),
                pltpu.SemaphoreType.DMA((3,)),
                pltpu.SemaphoreType.DMA((3,)),
            ],
            compiler_params=pltpu.CompilerParams(vmem_limit_bytes=63 * 1024 * 1024),
            cost_estimate=pl.CostEstimate(
                flops=2 * m_rows * k_all * (n_all - n1), bytes_accessed=6 * m_rows * k_all, transcendentals=0),
            name="rest",
        )(a, bh, c1)

    spec = P("fsdp", None)
    return jax.shard_map(local_fn, mesh=mesh, in_specs=(spec, spec), out_specs=spec, check_vma=False)
```

time: 318 us -> 314 us (0.987)
  Pallas kernels: 317 us -> 313 us
    pallas_call x1, Pallas kernels: 152 us -> 146 us  [local_fn(): pl.pallas_call(lambda *refs: _rest_kernel(n1, bn, *refs), out_shape=jax.S...]
where the time goes in v2:
time: 314 us
  Pallas kernels  313 us (100%)
    pallas_call x1, Pallas kernels, local_fn(): pl.pallas_call(lambda *refs: _gather_kernel(n1, *refs), out_shape=(jax.Sh...  167 us
    pallas_call x1, Pallas kernels, local_fn(): pl.pallas_call(lambda *refs: _rest_kernel(n1, bn, *refs), out_shape=jax.S...  146 us

profile of v2, /device:TPU:0, one launch (start us, length us, event | category | flops | bytes accessed | tf_op | source)
XLA Modules:
  0.0 313.6 jit_solution(11804413505738230653)
XLA Ops:
  0.0 166.9 %gather_half.1 = (bf16[8192,2048]{1,0:T(8,128)(2,1)}, bf16[4096,2048]{1,0:T(8,128)(2,1)}) custom-call(bf16[8192,4096]{1,0:T(8,128)(2,1)} %refs_0_.3, bf16[512,4096]{1,0:T(8,128)(2,1)} %refs_1_.1), custom_call_target="tpu_custom_call" | custom-call | flops 137438953472 | bytes 201326592 | tf_op jit(solution)/shard_map/gather_half/pallas_call | solution.py:493
  166.9 146.5 %rest.1 = bf16[8192,4096]{1,0:T(8,128)(2,1)} custom-call(bf16[8192,4096]{1,0:T(8,128)(2,1)} %refs_0_.3, bf16[4096,2048]{1,0:T(8,128)(2,1)} %get-tuple-element.7.refs_1_, bf16[8192,2048]{1,0:T(8,128)(2,1)} %get-tuple-element.8.refs_2_), custom_call_target="tpu_custom_call" | custom-call | flops 137438953472 | bytes 201326592 | tf_op jit(solution)/shard_map/rest/pallas_call | solution.py:517

commit v3 on v2

--- a/solution.py
+++ b/solution.py
@@ -41,8 +41,11 @@
     for dev in (partner, dev_x, dev_y):
         pl.semaphore_signal(barrier, inc=1, device_id=(dev,), device_id_type=MESH)
 
-    own_v = pltpu.make_async_copy(
-        b_hbm.at[:, pl.ds(0, n1)], bv.at[pl.ds(pl.multiple_of(core * depth, depth), depth), :], lsem.at[0])
+    def own_v(first):
+        col, width, k = (0, JW, 0) if first else (JW, n1 - JW, 5)
+        rows = pl.ds(pl.multiple_of(core * depth, depth), depth)
+        return pltpu.make_async_copy(b_hbm.at[:, pl.ds(col, width)], bv.at[rows, pl.ds(col, width)], lsem.at[k])
+
     wide = n1 - 2 * JW
 
     def own_h(k, out):
@@ -61,11 +64,9 @@
             asem.at[slot, place],
         )
 
-    own_v.start()
-    for m in range(8):
+    own_v(True).start()
+    for m in range(2):
         a_copy(m, 0, m % 2, m // 2).start()
-    for k in range(2):
-        own_h(k, False).start()
 
     pl.semaphore_wait(barrier, 3)
 
@@ -161,7 +162,12 @@
 
     stage_a(0)
     stage_a(1)
-    own_v.wait()
+    for m in range(2, 8):
+        a_copy(m, 0, m % 2, m // 2).start()
+    own_v(False).start()
+    for k in range(2):
+        own_h(k, False).start()
+    own_v(True).wait()
     landed(0, (KP,))
     landed(1, (KP,))
 
@@ -201,7 +207,7 @@
                 a_copy(2 * i + 2 + slot, 1, slot, 2 - place).start()
                 a_copy(2 * i + 2 + slot, 2, slot, 3 - place).start()
 
-        @pl.when(i == 1)
+        @pl.when(i == 2)
         def _():
             stage_c(0)
             stage_c(1)
@@ -246,12 +252,14 @@
         def _():
             a_copy(0, 1, 0, 1).start()
 
+        acc[pair(i), :] += dot(pair_of(i, slab), bv[3 * slab:, 0:JW])
+
         @pl.when(i >= 1)
         def _():
             for slot in range(2):
                 out_copy(2 * i - 2 + slot, 0, JW, slot).wait()
 
-        res = (acc[pair(i), :] + dot(pair_of(i, slab), bv[3 * slab:, 0:JW])).astype(BF16)
+        res = acc[pair(i), :].astype(BF16)
         obuf[:, :, 0:JW] = res.reshape(2, BM, JW)
         for slot in range(2):
             out_copy(2 * i + slot, 0, JW, slot).start()
@@ -265,10 +273,10 @@
     def g2_last(m, carry):
         slot, place = m % 2, 3 * (7 - m)
         a_copy(m, 3, 1, place).wait()
+        rows = pl.ds(pl.multiple_of(m * BM, BM), BM)
+        acc[rows, :] += dot(abuf[1, :, pl.ds(pl.multiple_of(place * slab, slab), slab)], bv[3 * slab:, 0:JW])
         out_copy(m - 2, 0, JW, slot).wait()
-        rows = pl.ds(pl.multiple_of(m * BM, BM), BM)
-        obuf[slot, :, 0:JW] = (acc[rows, :] + dot(
-            abuf[1, :, pl.ds(pl.multiple_of(place * slab, slab), slab)], bv[3 * slab:, 0:JW])).astype(BF16)
+        obuf[slot, :, 0:JW] = acc[rows, :].astype(BF16)
         out_copy(m, 0, JW, slot).start()
         return carry
 
@@ -299,9 +307,7 @@
 
         @pl.when(m % 2 == 1)
         def _():
-            @pl.when(m < nm - 1)
-            def _():
-                stage_b(5 + h)
+            stage_b(5 + h)
             stage_a(7 + h)
 
         @pl.when(m == nm - 1)
@@ -318,21 +324,22 @@
         out_copy(m, JW, JW, slot).start()
         return carry
 
+    own_v(False).wait()
     lax.fori_loop(0, nm, job1, 0)
     for t in range(4, 8):
         landed(t, (KP, KXP, KYP, KDYP, KDXP))
     def job2(m, carry):
         slot = tiles(m, m, m == nm - 1)
-        stage_b(8 + m)
+        stage_b(9 + m)
         stage_a(11 + m)
 
-        @pl.when(m >= 2)
-        def _():
-            stage_c(6 + m)
+        @pl.when(m >= 1)
+        def _():
+            stage_c(7 + m)
 
         @pl.when(m == nm - 1)
         def _():
-            stage_c(14)
+            stage_c(15)
 
         @pl.when(m < 2)
         def _():
@@ -347,7 +354,6 @@
         return carry
 
     lax.fori_loop(0, nm, job2, 0)
-    stage_c(15)
 
     def rest(t, carry):
         for kind in (KP, KXP, KYP, KDYP, KDXP):
@@ -504,7 +510,7 @@
                 pltpu.SemaphoreType.DMA((9, pieces)),
                 pltpu.SemaphoreType.DMA((2, 4)),
                 pltpu.SemaphoreType.DMA((2,)),
-                pltpu.SemaphoreType.DMA((5,)),
+                pltpu.SemaphoreType.DMA((6,)),
             ],
             compiler_params=pltpu.CompilerParams(
                 collective_id=0, has_side_effects=True, vmem_limit_bytes=63 * 1024 * 1024),

time: 314 us -> 308 us (0.981)
  Pallas kernels: 313 us -> 307 us
    pallas_call x1, Pallas kernels: 167 us -> 161 us  [local_fn(): pl.pallas_call(lambda *refs: _gather_kernel(n1, *refs), out_shape=(jax.Sh...]
where the time goes in v3:
time: 308 us
  Pallas kernels  307 us (100%)
    pallas_call x1, Pallas kernels, local_fn(): pl.pallas_call(lambda *refs: _gather_kernel(n1, *refs), out_shape=(jax.Sh...  161 us
    pallas_call x1, Pallas kernels, local_fn(): pl.pallas_call(lambda *refs: _rest_kernel(n1, bn, *refs), out_shape=jax.S...  146 us

profile of v3, /device:TPU:0, one launch (start us, length us, event | category | flops | bytes accessed | tf_op | source)
XLA Modules:
  0.0 307.6 jit_solution(4318872707984171787)
XLA Ops:
  0.0 160.9 %gather_half.1 = (bf16[8192,2048]{1,0:T(8,128)(2,1)}, bf16[4096,2048]{1,0:T(8,128)(2,1)}) custom-call(bf16[8192,4096]{1,0:T(8,128)(2,1)} %refs_0_.3, bf16[512,4096]{1,0:T(8,128)(2,1)} %refs_1_.1), custom_call_target="tpu_custom_call" | custom-call | flops 137438953472 | bytes 201326592 | tf_op jit(solution)/shard_map/gather_half/pallas_call | solution.py:499
  160.9 146.5 %rest.1 = bf16[8192,4096]{1,0:T(8,128)(2,1)} custom-call(bf16[8192,4096]{1,0:T(8,128)(2,1)} %refs_0_.3, bf16[4096,2048]{1,0:T(8,128)(2,1)} %get-tuple-element.7.refs_1_, bf16[8192,2048]{1,0:T(8,128)(2,1)} %get-tuple-element.8.refs_2_), custom_call_target="tpu_custom_call" | custom-call | flops 137438953472 | bytes 201326592 | tf_op jit(solution)/shard_map/rest/pallas_call | solution.py:523

commit v4 on v3

--- a/solution.py
+++ b/solution.py
@@ -79,8 +79,9 @@
             base = (2 * r + c) if in_v else (2 * chip_at(r) + c)
             return pl.ds(pl.multiple_of(base * depth + first, half), size)
 
-        own_src = b_hbm.at[:, cols_b]
         at = lambda r, c, first=0, size=depth: buf.at[rows(r, c, first, size), cols]
+        first = isinstance(t, int) and t < JW // CW
+        own_src = at(0, core) if first else b_hbm.at[:, cols_b]
         if kind == KP:
             src, dst, dev = own_src, at(0, core), partner
         elif kind == KX:
@@ -145,10 +146,15 @@
         each(t, lambda in_v: [copy(kind, t, in_v).wait_recv() for kind in kinds])
 
     def out_copy(m, col, width, slot):
-        return pltpu.make_async_copy(
-            obuf.at[slot, :, pl.ds(0, width)],
+        half = 0 if width != JW else (m // 2) % 2
+        first = 0 if width != JW else pl.multiple_of(half * JW, JW)
+        return pltpu.make_async_copy(
+            obuf.at[slot, :, pl.ds(first, width)],
             c1_hbm.at[pl.ds(pl.multiple_of(m * BM, BM), BM), pl.ds(col, width)],
-            osem.at[slot])
+            osem.at[slot, half])
+
+    def half_of(m):
+        return pl.ds(pl.multiple_of(((m // 2) % 2) * JW, JW), JW)
 
     def dot(x, y):
         return jnp.dot(x, y, preferred_element_type=F32)
@@ -160,6 +166,7 @@
         x = abuf[:, :, pl.ds(pl.multiple_of(place * slab, slab), width)]
         return x.reshape(2 * BM, width)
 
+    own_v(True).wait()
     stage_a(0)
     stage_a(1)
     for m in range(2, 8):
@@ -167,7 +174,6 @@
     own_v(False).start()
     for k in range(2):
         own_h(k, False).start()
-    own_v(True).wait()
     landed(0, (KP,))
     landed(1, (KP,))
 
@@ -252,21 +258,20 @@
         def _():
             a_copy(0, 1, 0, 1).start()
 
-        acc[pair(i), :] += dot(pair_of(i, slab), bv[3 * slab:, 0:JW])
-
-        @pl.when(i >= 1)
+        @pl.when(i == 2)
         def _():
             for slot in range(2):
-                out_copy(2 * i - 2 + slot, 0, JW, slot).wait()
-
-        res = acc[pair(i), :].astype(BF16)
-        obuf[:, :, 0:JW] = res.reshape(2, BM, JW)
+                out_copy(slot, 0, JW, slot).wait()
+
+        res = (acc[pair(i), :] + dot(pair_of(i, slab), bv[3 * slab:, 0:JW])).astype(BF16)
+        obuf[:, :, half_of(2 * i)] = res.reshape(2, BM, JW)
         for slot in range(2):
             out_copy(2 * i + slot, 0, JW, slot).start()
         return carry
 
     lax.fori_loop(0, nm // 2 - 1, g2, 0)
     a_copy(0, 2, 0, 2).start()
+    stage_c(3)
     stage_b(4)
     stage_a(6)
 
@@ -274,9 +279,9 @@
         slot, place = m % 2, 3 * (7 - m)
         a_copy(m, 3, 1, place).wait()
         rows = pl.ds(pl.multiple_of(m * BM, BM), BM)
-        acc[rows, :] += dot(abuf[1, :, pl.ds(pl.multiple_of(place * slab, slab), slab)], bv[3 * slab:, 0:JW])
-        out_copy(m - 2, 0, JW, slot).wait()
-        obuf[slot, :, 0:JW] = acc[rows, :].astype(BF16)
+        out_copy(m - 4, 0, JW, slot).wait()
+        obuf[slot, :, half_of(m)] = (acc[rows, :] + dot(
+            abuf[1, :, pl.ds(pl.multiple_of(place * slab, slab), slab)], bv[3 * slab:, 0:JW])).astype(BF16)
         out_copy(m, 0, JW, slot).start()
         return carry
 
@@ -301,7 +306,7 @@
         slot = tiles(m, m, None)
         h = m // 2
 
-        @pl.when(m % 2 == 0)
+        @pl.when(jnp.logical_and(m % 2 == 0, m > 0))
         def _():
             stage_c(3 + h)
 
@@ -320,7 +325,7 @@
                 landed(t, (KP, KXP, KYP, KDYP, KDXP))
 
         out_copy(m, JW, JW, slot).wait()
-        obuf[slot, :, 0:JW] = dot(abuf[slot], bv[:, JW:2 * JW]).astype(BF16)
+        obuf[slot, :, half_of(m)] = dot(abuf[slot], bv[:, JW:2 * JW]).astype(BF16)
         out_copy(m, JW, JW, slot).start()
         return carry
 
@@ -344,6 +349,7 @@
         @pl.when(m < 2)
         def _():
             out_copy(m, JW, JW, slot).wait()
+            out_copy(m + 2, JW, JW, slot).wait()
 
         @pl.when(m >= 2)
         def _():
@@ -509,7 +515,7 @@
                 pltpu.SemaphoreType.DMA((9, pieces)),
                 pltpu.SemaphoreType.DMA((9, pieces)),
                 pltpu.SemaphoreType.DMA((2, 4)),
-                pltpu.SemaphoreType.DMA((2,)),
+                pltpu.SemaphoreType.DMA((2, 2)),
                 pltpu.SemaphoreType.DMA((6,)),
             ],
             compiler_params=pltpu.CompilerParams(

time: 308 us -> 308 us (level)
  no operation moved by 1% of the time
where the time goes in v4:
time: 308 us; the launch traced here: 307 us
  Pallas kernels  307 us (100%)
    pallas_call x1, Pallas kernels, local_fn(): pl.pallas_call(lambda *refs: _gather_kernel(n1, *refs), out_shape=(jax.Sh...  160 us
    pallas_call x1, Pallas kernels, local_fn(): pl.pallas_call(lambda *refs: _rest_kernel(n1, bn, *refs), out_shape=jax.S...  146 us

profile of v4, /device:TPU:0, one launch (start us, length us, event | category | flops | bytes accessed | tf_op | source)
XLA Modules:
  0.0 307.1 jit_solution(8142856164261738564)
XLA Ops:
  0.0 160.4 %gather_half.1 = (bf16[8192,2048]{1,0:T(8,128)(2,1)}, bf16[4096,2048]{1,0:T(8,128)(2,1)}) custom-call(bf16[8192,4096]{1,0:T(8,128)(2,1)} %refs_0_.3, bf16[512,4096]{1,0:T(8,128)(2,1)} %refs_1_.1), custom_call_target="tpu_custom_call" | custom-call | flops 137438953472 | bytes 201326592 | tf_op jit(solution)/shard_map/gather_half/pallas_call | solution.py:505
  160.4 146.5 %rest.1 = bf16[8192,4096]{1,0:T(8,128)(2,1)} custom-call(bf16[8192,4096]{1,0:T(8,128)(2,1)} %refs_0_.3, bf16[4096,2048]{1,0:T(8,128)(2,1)} %get-tuple-element.7.refs_1_, bf16[8192,2048]{1,0:T(8,128)(2,1)} %get-tuple-element.8.refs_2_), custom_call_target="tpu_custom_call" | custom-call | flops 137438953472 | bytes 201326592 | tf_op jit(solution)/shard_map/rest/pallas_call | solution.py:529
